TPU v7x, 32 devices: a whole 2x2x4 slice. The times are simulated.
32 devices in a mesh: frag: 2 (over x), grid: 16 (over z, y, core).
Axes of the slice: x: 2, y: 2, z: 4, core: 2. Of those that a mesh axis runs over, the one named last changes fastest.
Arguments:
- psi: float32 [16384, 640], P(('frag', 'grid')), parts along dimension 0
- order: int32 [10], P('frag'), parts along dimension 0, may hold values from 0 to 4, each once
Outputs:
- orthonormal: float32 [16384, 640], P(('frag', 'grid')), parts along dimension 0
There are 2 independent parts, one for each index of `frag`. A program takes and returns all parts, laid end to end along the dimension named above; each array names one. Nothing has to cross between parts.
All inputs are finite; a program needn't handle non-finite values.
Results may differ from a plain program's by a relative error of at most 0.00012.
Values sent between devices are 32-bit elements; how exact they have to be, the bound alone decides.
A program may use at most 64 MiB of HBM per device.

v0:
```python
import jax
import jax.numpy as jnp
from jax import lax
from jax.sharding import PartitionSpec as P

BLOCK = 128
NBLK = 5


def contract(left, right):
    return lax.dot_general(
        left,
        right,
        (((0,), (0,)), ((), ())),
        precision=lax.Precision.HIGHEST,
        preferred_element_type=jnp.float32,
    )


def matmul(left, right):
    return jnp.dot(left, right, precision=lax.Precision.HIGHEST, preferred_element_type=jnp.float32)


def factor_inverse(gram, width):
    lower = jnp.linalg.cholesky(gram)
    return lax.linalg.triangular_solve(
        lower, jnp.eye(width, dtype=gram.dtype), left_side=True, lower=True
    )


def local(psi, order):
    scale = jnp.float32(1.0 / (psi.shape[0] * lax.axis_size("grid")))
    rows = psi.shape[0]
    reordered = jnp.take(psi.reshape(rows, NBLK, BLOCK), order, axis=1).reshape(rows, NBLK * BLOCK)
    whole = lax.psum(contract(reordered, reordered) * scale, "grid")
    inverse = factor_inverse(whole, NBLK * BLOCK)
    basis = matmul(reordered, inverse.T).reshape(rows, NBLK, BLOCK)
    result = jnp.zeros((rows, NBLK, BLOCK), psi.dtype).at[:, order, :].set(basis)
    return result.reshape(rows, NBLK * BLOCK)


def solution(mesh):
    in_specs = (P(("frag", "grid"), None), P("frag"))
    out_specs = P(("frag", "grid"), None)
    return jax.shard_map(local, mesh=mesh, in_specs=in_specs, out_specs=out_specs, check_vma=False)
```

profile of v0, /device:TPU:0, one launch (start us, length us, event | category | flops | bytes accessed | tf_op | source)
XLA Modules:
  0.0 329.6 jit_solution(3840453212950638409)
XLA Ops:
  6.5 0.7 compare_select_fusion
  7.2 0.7 compare_and_fusion
  7.9 1.7 copy.5
  10.0 0.6 gather_fusion
  10.6 1.2 select_bitcast_fusion
  11.9 1.7 copy.7
  13.6 4.5 %convolution_multiply_fusion = f32[640,640]{0,1:T(8,128)} fusion(f32[512,640]{0,1:T(8,128)S(1)} %bitcast.79), kind=kOutput, calls=%fused_computation.9 | convolution fusion | flops 2516992000 | bytes 2949120 | tf_op jit(solution)/shard_map/dot_general | solution.py:11
  18.1 0.9 iota_compare_fusion
  19.0 1.3 fusion.20
  20.2 97.1 %all-reduce.3.cloned.1.call-done = f32[640,640]{0,1:T(8,128)} async-done(((f32[640,640]{0,1:T(8,128)}), f32[640,640]{0,1:T(8,128)}) %all-reduce.3.cloned.1.call-update) | async-done | bytes 1638416 | tf_op jit(solution)/shard_map/psum | solution.py:35
  117.3 3.0 copy.9
  120.3 1.6 fusion
  121.9 1.2 copy-done.1
  123.1 11.7 %cholesky.133 = f32[128,128]{1,0:T(8,128)S(1)} custom-call(f32[128,128]{1,0:T(8,128)S(1)} %cholesky.340), custom_call_target="Cholesky" | custom-call | tf_op jit(solution)/shard_map/jit(cholesky)/cholesky | solution.py:25
  134.9 9.8 %custom-call.38 = f32[1,128,128]{1,2,0:T(8,128)S(1)} custom-call(f32[1,128,128]{2,1,0:T(8,128)S(1)} %get-tuple-element.35), custom_call_target="InvertDiagBlocksLowerTriangular" | custom-call | tf_op jit(solution)/shard_map/jit(cholesky)/cholesky | solution.py:25
  144.8 1.3 constant_dynamic-update-slice_fusion.8
  146.1 1.3 convolution_subtract_fusion.3
  147.5 11.7 %cholesky.272 = f32[128,128]{1,0:T(8,128)S(1)} custom-call(f32[128,128]{1,0:T(8,128)S(1)} %cholesky.344), custom_call_target="Cholesky" | custom-call | tf_op jit(solution)/shard_map/jit(cholesky)/cholesky | solution.py:25
  159.2 10.0 %custom-call.39 = f32[1,128,128]{1,2,0:T(8,128)S(1)} custom-call(f32[1,128,128]{2,1,0:T(8,128)S(1)} %get-tuple-element.32), custom_call_target="InvertDiagBlocksLowerTriangular" | custom-call | tf_op jit(solution)/shard_map/jit(cholesky)/cholesky | solution.py:25
  169.5 1.4 convolution_subtract_fusion.4
  171.0 11.7 %cholesky.293 = f32[128,128]{1,0:T(8,128)S(1)} custom-call(f32[128,128]{1,0:T(8,128)S(1)} %cholesky.349), custom_call_target="Cholesky" | custom-call | tf_op jit(solution)/shard_map/jit(cholesky)/cholesky | solution.py:25
  182.7 0.6 compare_reduce_fusion.2
  183.4 9.8 %custom-call.40 = f32[1,128,128]{1,2,0:T(8,128)S(1)} custom-call(f32[1,128,128]{2,1,0:T(8,128)S(1)} %get-tuple-element.29), custom_call_target="InvertDiagBlocksLowerTriangular" | custom-call | tf_op jit(solution)/shard_map/jit(cholesky)/cholesky | solution.py:25
  193.4 1.4 convolution_subtract_fusion.5
  194.8 12.1 %cholesky.312 = f32[128,128]{1,0:T(8,128)S(1)} custom-call(f32[128,128]{1,0:T(8,128)S(1)} %cholesky.354), custom_call_target="Cholesky" | custom-call | tf_op jit(solution)/shard_map/jit(cholesky)/cholesky | solution.py:25
  207.0 0.7 compare_reduce_fusion.1
  207.6 9.8 %custom-call.41 = f32[1,128,128]{1,2,0:T(8,128)S(1)} custom-call(f32[1,128,128]{2,1,0:T(8,128)S(1)} %get-tuple-element.26), custom_call_target="InvertDiagBlocksLowerTriangular" | custom-call | tf_op jit(solution)/shard_map/jit(cholesky)/cholesky | solution.py:25
  217.7 1.2 convolution_subtract_fusion.6
  218.9 11.7 %cholesky.329 = f32[128,128]{1,0:T(8,128)S(1)} custom-call(f32[128,128]{1,0:T(8,128)S(1)} %convolution_subtract_fusion.6), custom_call_target="Cholesky" | custom-call | tf_op jit(solution)/shard_map/jit(cholesky)/cholesky | solution.py:25
  230.6 0.7 compare_reduce_fusion
  231.3 0.7 compare_reduce_fusion.3
  235.1 1.3 select_select_fusion
  236.4 17.1 %while.1 = (s32[]{:T(128)}, f32[640,640]{1,0:T(8,128)}, s32[5,2]{0,1:T(2,128)S(1)}, f32[5,128,128]{2,1,0:T(8,128)}, s32[]{:T(128)}) while((s32[]{:T(128)}, f32[640,640]{1,0:T(8,128)}, s32[5,2]{0,1:T(2,128)S(1)}, f32[5,128,128]{2,1,0:T(8,128)}, s32[]{:T(128)}) %tuple.33), condition=%wide.while_cond, body=%wide.while_body.sunk | while | flops 2 | bytes 132705 | solution.py:26
  237.0 2.8 bitcast_dynamic-update-slice_fusion.2
  240.4 2.8 bitcast_dynamic-update-slice_fusion.2
  243.3 0.5 fusion.60
  243.8 2.8 bitcast_dynamic-update-slice_fusion.2
  247.3 2.8 bitcast_dynamic-update-slice_fusion.2
  250.7 2.7 bitcast_dynamic-update-slice_fusion.2
  253.4 50.2 %custom-call.42 = f32[5,128,128]{1,2,0:T(8,128)S(1)} custom-call(f32[5,128,128]{2,1,0:T(8,128)} %get-tuple-element.12), custom_call_target="InvertDiagBlocksLowerTriangular" | custom-call | tf_op jit(solution)/shard_map/triangular_solve | solution.py:26
  303.7 1.1 constant_dynamic-update-slice_fusion.3
  304.8 1.4 convolution_subtract_fusion.1
  306.7 1.4 convolution_subtract_fusion
  308.6 1.8 convolution_subtract_fusion.2
  310.9 1.9 fusion.9
  313.3 6.4 %convolution_bitcast_fusion = f32[5,512,128]{2,1,0:T(8,128)S(1)} fusion(f32[512,640,1]{0,1,2:T(8,128)S(1)} %bitcast.80, f32[5,128,640]{2,1,0:T(8,128)S(1)} %bitcast.83), kind=kOutput, calls=%fused_computation.10 | convolution fusion | flops 2516582400 | bytes 4259840 | tf_op jit(solution)/shard_map/dot_general | solution.py:21
  319.8 0.9 scatter_fusion
  321.1 1.5 copy.12
  (40 shorter events, 6.4 us)
Async XLA Ops:
  6.5 110.8 %all-reduce.3.cloned.1.call-start = ((), (), s32[]{:S(2)}) async-start(), calls=%async_computation | async-start | bytes 3276800 | tf_op jit(solution)/shard_map/psum | solution.py:35
  117.3 3.0 copy-start
  121.9 1.2 copy-start.1
  253.4 53.3 %copy-start.2 = (f32[640,640]{1,0:T(8,128)S(1)}, f32[640,640]{1,0:T(8,128)}, u32[]{:S(2)}) copy-start(f32[640,640]{1,0:T(8,128)} %fusion.20) | copy-start | bytes 4915204
Sparse Core Ops, SparseCore 0:
  18.2 99.0 all-reduce.2
where the time goes:
time: 334 us; the launch traced here: 330 us
  other arithmetic  159 us (48%)
  waiting for transfers between devices  97.1 us (29%)
  local copies, waits for them, and re-layouts  28.7 us (9%)
  matrix products  27.8 us (8%)
  between operations  16.9 us (5%)
    another operation x18, other arithmetic, factor_inverse(): lower = jnp.linalg.cholesky(gram)  101 us
    psum x1, waiting for transfers between devices, local(): whole = lax.psum(contract(reordered, reordered) * scale, 'grid')  97.1 us
    another operation x3, other arithmetic, factor_inverse(): lax.linalg.triangular_solve(lower, jnp.eye(width, dtype=gram.dtype), left...  51.5 us
    another operation x15, local copies, waits for them, and re-layouts  17.1 us
    another operation x9, matrix products, factor_inverse(): lax.linalg.triangular_solve(lower, jnp.eye(width, dtype=gram.dtype), left...  9.56 us
    another operation x8, matrix products, factor_inverse(): lower = jnp.linalg.cholesky(gram)  7.43 us
  transfers between devices with their start and end apart: 1, of which 1 were waited for; matrix products, arithmetic and copies ran while one was open for 1% of the time, Pallas kernels for 0%

commit v1 on v0

--- a/solution.py
+++ b/solution.py
@@ -32,7 +32,8 @@
     scale = jnp.float32(1.0 / (psi.shape[0] * lax.axis_size("grid")))
     rows = psi.shape[0]
     reordered = jnp.take(psi.reshape(rows, NBLK, BLOCK), order, axis=1).reshape(rows, NBLK * BLOCK)
-    whole = lax.psum(contract(reordered, reordered) * scale, "grid")
+    row_data = contract(reordered, reordered) * scale
+    whole = lax.all_gather(row_data, "grid").sum(axis=0)
     inverse = factor_inverse(whole, NBLK * BLOCK)
     basis = matmul(reordered, inverse.T).reshape(rows, NBLK, BLOCK)
     result = jnp.zeros((rows, NBLK, BLOCK), psi.dtype).at[:, order, :].set(basis)

time: 334 us -> 382 us (1.14)
  waiting for transfers between devices: 97.1 us -> 134 us
  other arithmetic: 159 us -> 170 us
    all_gather x0 -> x1, waiting for transfers between devices: none -> 134 us  [local(): whole = lax.all_gather(row_data, 'grid').sum(axis=0)]
    psum x1 -> x0, waiting for transfers between devices: 97.1 us -> none  [local(): whole = lax.psum(contract(reordered, reordered) * scale, 'grid')]
    reduce_sum x0 -> x1, other arithmetic: none -> 10.5 us  [local(): whole = lax.all_gather(row_data, 'grid').sum(axis=0)]
where the time goes in v1:
time: 382 us; the launch traced here: 377 us
  other arithmetic  170 us (45%)
  waiting for transfers between devices  134 us (35%)
  local copies, waits for them, and re-layouts  27.9 us (7%)
  matrix products  27.8 us (7%)
  between operations  17.1 us (4%)
    all_gather x1, waiting for transfers between devices, local(): whole = lax.all_gather(row_data, 'grid').sum(axis=0)  134 us
    another operation x18, other arithmetic, factor_inverse(): lower = jnp.linalg.cholesky(gram)  101 us
    another operation x3, other arithmetic, factor_inverse(): lax.linalg.triangular_solve(lower, jnp.eye(width, dtype=gram.dtype), left...  51.6 us
    another operation x15, local copies, waits for them, and re-layouts  17.5 us
    reduce_sum x1, other arithmetic, local(): whole = lax.all_gather(row_data, 'grid').sum(axis=0)  10.5 us
    another operation x9, matrix products, factor_inverse(): lax.linalg.triangular_solve(lower, jnp.eye(width, dtype=gram.dtype), left...  9.56 us
  transfers between devices with their start and end apart: 1, of which 1 were waited for; matrix products, arithmetic and copies ran while one was open for 1% of the time, Pallas kernels for 0%

profile of v1, /device:TPU:0, one launch (start us, length us, event | category | flops | bytes accessed | tf_op | source)
XLA Modules:
  0.0 376.6 jit_solution(6757151556197636187)
XLA Ops:
  6.5 0.7 compare_select_fusion
  7.2 0.7 compare_and_fusion
  7.9 1.7 copy.11
  10.0 0.6 gather_fusion
  10.6 1.2 select_bitcast_fusion
  11.9 1.7 copy.13
  13.6 4.5 %convolution_multiply_fusion = f32[640,640]{1,0:T(8,128)} fusion(f32[512,640]{0,1:T(8,128)S(1)} %bitcast.81), kind=kOutput, calls=%fused_computation.9 | convolution fusion | flops 2516992000 | bytes 2949120 | tf_op jit(solution)/shard_map/dot_general | solution.py:11
  18.1 0.9 iota_compare_fusion
  19.0 1.3 fusion.20
  20.3 134.2 %all-gather.3.cloned.1.call-done = f32[10240,640]{1,0:T(8,128)} async-done(((f32[640,640]{1,0:T(8,128)}), f32[10240,640]{1,0:T(8,128)}) %all-gather.3.cloned.1.call-update) | async-done | bytes 26214416 | tf_op jit(solution)/shard_map/all_gather | solution.py:36
  154.4 10.5 %reduce_sum.9 = f32[640,640]{1,0:T(8,128)S(1)} reduce(f32[16,640,640]{2,1,0:T(8,128)} %bitcast.80, f32[]{:T(128)} %constant.184.clone.1), dimensions={0}, to_apply=%region_0.1 | reduce | flops 6144000 | bytes 27852804 | tf_op jit(solution)/shard_map/reduce_sum | solution.py:36
  164.9 1.9 copy.14
  166.8 1.6 fusion
  168.4 1.2 copy-done
  169.6 11.7 %cholesky.133 = f32[128,128]{1,0:T(8,128)S(1)} custom-call(f32[128,128]{1,0:T(8,128)S(1)} %cholesky.340), custom_call_target="Cholesky" | custom-call | tf_op jit(solution)/shard_map/jit(cholesky)/cholesky | solution.py:25
  181.4 9.8 %custom-call.38 = f32[1,128,128]{1,2,0:T(8,128)S(1)} custom-call(f32[1,128,128]{2,1,0:T(8,128)S(1)} %get-tuple-element.35), custom_call_target="InvertDiagBlocksLowerTriangular" | custom-call | tf_op jit(solution)/shard_map/jit(cholesky)/cholesky | solution.py:25
  191.2 1.3 constant_dynamic-update-slice_fusion.8
  192.6 1.3 convolution_subtract_fusion.3
  193.9 11.7 %cholesky.272 = f32[128,128]{1,0:T(8,128)S(1)} custom-call(f32[128,128]{1,0:T(8,128)S(1)} %cholesky.344), custom_call_target="Cholesky" | custom-call | tf_op jit(solution)/shard_map/jit(cholesky)/cholesky | solution.py:25
  205.7 10.0 %custom-call.39 = f32[1,128,128]{1,2,0:T(8,128)S(1)} custom-call(f32[1,128,128]{2,1,0:T(8,128)S(1)} %get-tuple-element.32), custom_call_target="InvertDiagBlocksLowerTriangular" | custom-call | tf_op jit(solution)/shard_map/jit(cholesky)/cholesky | solution.py:25
  216.0 1.4 convolution_subtract_fusion.4
  217.4 11.7 %cholesky.293 = f32[128,128]{1,0:T(8,128)S(1)} custom-call(f32[128,128]{1,0:T(8,128)S(1)} %cholesky.349), custom_call_target="Cholesky" | custom-call | tf_op jit(solution)/shard_map/jit(cholesky)/cholesky | solution.py:25
  229.1 0.7 compare_reduce_fusion.2
  229.8 9.8 %custom-call.40 = f32[1,128,128]{1,2,0:T(8,128)S(1)} custom-call(f32[1,128,128]{2,1,0:T(8,128)S(1)} %get-tuple-element.29), custom_call_target="InvertDiagBlocksLowerTriangular" | custom-call | tf_op jit(solution)/shard_map/jit(cholesky)/cholesky | solution.py:25
  239.9 1.4 convolution_subtract_fusion.5
  241.3 12.1 %cholesky.312 = f32[128,128]{1,0:T(8,128)S(1)} custom-call(f32[128,128]{1,0:T(8,128)S(1)} %cholesky.354), custom_call_target="Cholesky" | custom-call | tf_op jit(solution)/shard_map/jit(cholesky)/cholesky | solution.py:25
  253.4 0.7 compare_reduce_fusion.1
  254.1 9.8 %custom-call.41 = f32[1,128,128]{1,2,0:T(8,128)S(1)} custom-call(f32[1,128,128]{2,1,0:T(8,128)S(1)} %get-tuple-element.26), custom_call_target="InvertDiagBlocksLowerTriangular" | custom-call | tf_op jit(solution)/shard_map/jit(cholesky)/cholesky | solution.py:25
  264.1 1.2 convolution_subtract_fusion.6
  265.4 11.7 %cholesky.329 = f32[128,128]{1,0:T(8,128)S(1)} custom-call(f32[128,128]{1,0:T(8,128)S(1)} %convolution_subtract_fusion.6), custom_call_target="Cholesky" | custom-call | tf_op jit(solution)/shard_map/jit(cholesky)/cholesky | solution.py:25
  277.1 0.7 compare_reduce_fusion
  277.8 0.7 compare_reduce_fusion.3
  281.7 1.3 select_select_fusion
  283.0 17.5 %while.1 = (s32[]{:T(128)}, f32[640,640]{1,0:T(8,128)}, s32[5,2]{0,1:T(2,128)S(1)}, f32[5,128,128]{2,1,0:T(8,128)}, s32[]{:T(128)}) while((s32[]{:T(128)}, f32[640,640]{1,0:T(8,128)}, s32[5,2]{0,1:T(2,128)S(1)}, f32[5,128,128]{2,1,0:T(8,128)}, s32[]{:T(128)}) %tuple.33), condition=%wide.while_cond, body=%wide.while_body.sunk | while | flops 2 | bytes 132705 | solution.py:26
  283.6 2.9 bitcast_dynamic-update-slice_fusion.2
  287.1 2.9 bitcast_dynamic-update-slice_fusion.2
  290.6 2.9 bitcast_dynamic-update-slice_fusion.2
  294.1 2.9 bitcast_dynamic-update-slice_fusion.2
  297.6 2.8 bitcast_dynamic-update-slice_fusion.2
  300.5 50.2 %custom-call.42 = f32[5,128,128]{1,2,0:T(8,128)S(1)} custom-call(f32[5,128,128]{2,1,0:T(8,128)} %get-tuple-element.12), custom_call_target="InvertDiagBlocksLowerTriangular" | custom-call | tf_op jit(solution)/shard_map/triangular_solve | solution.py:26
  350.7 1.1 constant_dynamic-update-slice_fusion.3
  351.8 1.4 convolution_subtract_fusion.1
  353.8 1.4 convolution_subtract_fusion
  355.7 1.8 convolution_subtract_fusion.2
  357.9 1.9 fusion.9
  360.3 6.4 %convolution_bitcast_fusion = f32[5,512,128]{2,1,0:T(8,128)S(1)} fusion(f32[512,640,1]{0,1,2:T(8,128)S(1)} %bitcast.82, f32[5,128,640]{2,1,0:T(8,128)S(1)} %bitcast.85), kind=kOutput, calls=%fused_computation.10 | convolution fusion | flops 2516582400 | bytes 4259840 | tf_op jit(solution)/shard_map/dot_general | solution.py:21
  366.8 0.9 scatter_fusion
  368.1 1.5 copy.17
  (39 shorter events, 6.9 us)
Async XLA Ops:
  6.5 147.9 %all-gather.3.cloned.1.call-start = ((), (), s32[]{:S(2)}) async-start(), calls=%async_computation | async-start | bytes 27852800 | tf_op jit(solution)/shard_map/all_gather | solution.py:36
  168.4 1.2 copy-start
  300.5 53.3 %copy-start.1 = (f32[640,640]{1,0:T(8,128)S(1)}, f32[640,640]{1,0:T(8,128)}, u32[]{:S(2)}) copy-start(f32[640,640]{1,0:T(8,128)} %fusion.20) | copy-start | bytes 4915204
Sparse Core Ops, SparseCore 0:
  18.2 136.1 all-gather.2
